TPU v7x, 32 devices: a whole 2x2x4 slice. The times are simulated.
32 devices in a mesh: inner: 4 (over z), outer: 8 (over y, x, core).
Axes of the slice: x: 2, y: 2, z: 4, core: 2. Of those that a mesh axis runs over, the one named last changes fastest.
Arguments:
- inner_state: float32 [2, 16, 2048], P(None, 'inner', 'outer'), may hold values from -6 to 6
- outer_state: float32 [2, 640, 4096], P(None, 'inner', 'outer'), may hold values from -6 to 6
- energies: float32 [16, 2048], P('inner', 'outer'), may hold values from -2 to 2
- dipole: float32 [16, 2048, 2048], P('inner', 'outer'), may hold values from -0.125 to 0.125
- surface: float32 [16, 40, 2048], P('inner', None, 'outer'), may hold values from -0.125 to 0.125
- thresholds: float32 [640], P('inner'), may hold values from 0 to 2
- coupling_coef: float32 [16, 40, 40], P('inner'), may hold values from -1 to 1
- coupling_pattern: int32 [16, 40, 40], P('inner'), may hold values 0 or 1
- block_sizes: int32 [16], P('inner'), may hold values from 1 to 2048, 30720 in all
- field_strength: float32 [2], replicated, may hold values from 0.5 to 2
Outputs:
- inner_final: float32 [2, 16, 2048], P(None, 'inner', 'outer')
- outer_final: float32 [2, 640, 4096], P(None, 'inner', 'outer')
All inputs are finite; a program needn't handle non-finite values. No bound on the sum of `coupling_pattern` or of `block_sizes` on one device may be relied on, other than what follows from the above.
Results may differ from a plain program's by a relative error of at most 0.0001.
Values sent between devices are 32-bit elements; how exact they have to be, the bound alone decides.
A program may use at most 128 MiB of HBM per device.

v0:
```python
import jax
import jax.numpy as jnp
from jax import lax
from jax.sharding import PartitionSpec as P

STEPS = 2
ORDER = 4
kinetic_scale = 3.125
time_step = 0.1


def from_behind(block, axis, distance):
    devices = range(lax.axis_size(axis))
    route = [(i - distance, i) for i in devices if i - distance in devices]
    return lax.ppermute(block, axis, route)


def spread(shard, axis, root):
    mine = lax.axis_index(axis) == root
    return lax.psum(jnp.where(mine, shard, jnp.zeros_like(shard)), axis)


def with_halo(cells, sides, width):
    for axis, dim in sides:
        count = lax.axis_size(axis)
        ends = count - 1
        head = lax.slice_in_dim(cells, 0, width, axis=dim)
        tail = lax.slice_in_dim(cells, cells.shape[dim] - width, cells.shape[dim], axis=dim)
        cells = jnp.concatenate(
            [
                lax.ppermute(tail, axis, [(i, (i + 1) % count) for i in range(ends)]),
                cells,
                lax.ppermute(head, axis, [((i + 1) % count, i) for i in range(ends)]),
            ],
            axis=dim,
        )
    return cells


def reduce_partials(partial_terms, partial_boundary):
    own_terms = lax.psum_scatter(partial_terms, "outer", scatter_dimension=2, tiled=True)
    boundary = lax.psum(partial_boundary, "outer")
    return (own_terms, boundary)


def local(
    inner_state,
    outer_state,
    energies,
    dipole,
    surface,
    thresholds,
    coupling_coef,
    coupling_pattern,
    block_sizes,
    field_strength,
):
    highest = lax.Precision.HIGHEST
    blocks = dipole.shape[0]
    row_count = dipole.shape[1]
    channels = coupling_coef.shape[1]
    radial = outer_state.shape[2]
    sector_index = lax.axis_index("outer")
    row_index = sector_index * row_count + jnp.arange(row_count, dtype=jnp.int32)
    live_rows = (row_index[None, :] < block_sizes[:, None]).astype(jnp.float32)
    coupling = coupling_coef * coupling_pattern.astype(jnp.float32)
    first_sector = jnp.where(sector_index == 0, 1.0, 0.0).astype(jnp.float32)
    edge_mask = first_sector * (jnp.arange(radial, dtype=jnp.int32) == 0).astype(jnp.float32)
    prev_dipole, prev_coupling = from_behind((dipole[blocks - 1], coupling[blocks - 1]), "inner", 1)
    current = (inner_state * live_rows, outer_state)
    for time_index in range(STEPS):
        strength = field_strength[time_index]
        taylor_term = current
        accumulated = current
        for power in range(1, ORDER + 1):
            inner_part = taylor_term[0]
            outer_part = taylor_term[1]
            channel_grid = outer_part.reshape(2, blocks, channels, radial)
            next_first, next_channels = from_behind(
                (inner_part[:, 0], channel_grid[:, 0]), "inner", -1
            )
            extended = jnp.concatenate([inner_part, next_first[:, None]], axis=1)
            gathered = lax.all_gather(extended, "outer", axis=2, tiled=True)
            edge_values = spread(outer_part[:, :, 0], "outer", 0)
            forward = jnp.einsum("lij,plj->pli", dipole, gathered[:, 1:], precision=highest)
            grid_next = jnp.concatenate([channel_grid[:, 1:], next_channels[:, None]], axis=1)
            upward = jnp.einsum("lab,plbr->plar", coupling, grid_next, precision=highest)
            partial_boundary = jnp.einsum("lcs,pls->plc", surface, inner_part, precision=highest)
            prev_rows, prev_channels = from_behind(
                (inner_part[:, blocks - 1], channel_grid[:, blocks - 1]), "inner", 1
            )
            source_rows = jnp.concatenate([prev_rows[:, None], inner_part[:, : blocks - 1]], axis=1)
            source_blocks = jnp.concatenate([prev_dipole[None], dipole[: blocks - 1]], axis=0)
            partial_terms = jnp.einsum(
                "lji,plj->pli", source_blocks, source_rows, precision=highest
            )
            backward, boundary = reduce_partials(partial_terms, partial_boundary)
            source_grid = jnp.concatenate(
                [prev_channels[:, None], channel_grid[:, : blocks - 1]], axis=1
            )
            source_coupling = jnp.concatenate([prev_coupling[None], coupling[: blocks - 1]], axis=0)
            downward = jnp.einsum("lba,plbr->plar", source_coupling, source_grid, precision=highest)
            first_point = edge_values.reshape(2, blocks, channels)
            surf_term = jnp.einsum("lcs,plc->pls", surface, first_point, precision=highest)
            inner_image = live_rows * (
                energies * inner_part + strength * (forward + backward) - kinetic_scale * surf_term
            )
            padded = with_halo(outer_part, (("outer", 2),), 1)
            left_cells = (
                padded[:, :, :radial]
                + edge_mask[None, None, :] * boundary.reshape(2, blocks * channels)[:, :, None]
            )
            right_cells = padded[:, :, 2:]
            kinetic = kinetic_scale * (2.0 * outer_part - left_cells - right_cells)
            outer_image = (
                kinetic
                + thresholds[None, :, None] * outer_part
                + strength * (upward + downward).reshape(2, blocks * channels, radial)
            )
            inner_image, outer_image = (inner_image, outer_image)
            factor = time_step / power
            taylor_term = (
                factor * jnp.stack([inner_image[1], -inner_image[0]]),
                factor * jnp.stack([outer_image[1], -outer_image[0]]),
            )
            accumulated = (accumulated[0] + taylor_term[0], accumulated[1] + taylor_term[1])
        current = accumulated
    return (current[0], current[1])


def solution(mesh):
    placed = (
        P(None, "inner", "outer"),
        P(None, "inner", "outer"),
        P("inner", "outer"),
        P("inner", "outer", None),
        P("inner", None, "outer"),
        P("inner"),
        P("inner", None, None),
        P("inner", None, None),
        P("inner"),
        P(),
    )
    return jax.shard_map(
        local,
        mesh=mesh,
        in_specs=placed,
        out_specs=(P(None, "inner", "outer"), P(None, "inner", "outer")),
        check_vma=False,
    )
```

profile of v0, /device:TPU:12, one launch (start us, length us, event | category | flops | bytes accessed | tf_op | source)
XLA Modules:
  0.0 834.8 jit_solution(18084127534141652575)
XLA Ops:
  34.9 12.6 %all-reduce.7 = (f32[2,160]{1,0:T(2,128)}, f32[2,4,40]{2,0,1:T(2,128)S(1)}) all-reduce(f32[2,160]{1,0:T(2,128)S(1)} %mul.616, f32[2,4,40]{2,0,1:T(2,128)S(1)} %copy.69), channel_id=1, replica_groups=mesh['inner'=4,'outer'=8] {'outer'}, use_global_device_ids=true, to_apply=%region_3.4 | all-reduce | flops 640 | bytes 5120 | tf_op jit(solution)/shard_map/psum | solution.py:42
  59.9 8.3 all_gather.24
  97.4 7.4 convolution_bitcast_fusion.7
  117.4 30.5 %reduce-scatter.25.cloned.1.call-done = f32[256,8]{1,0:T(8,128)} async-done(((f32[2048,8]{1,0:T(8,128)}), f32[256,8]{1,0:T(8,128)}) %reduce-scatter.25.cloned.1.call-update) | async-done | bytes 8208
  151.2 9.8 %fusion.55 = f32[2,4,256]{2,0,1:T(2,128)S(1)} fusion(f32[2,4,256]{2,0,1:T(2,128)S(1)} %fusion.63, f32[2,4,256]{2,0,1:T(2,128)S(1)} %copy.138, f32[2,5,2048]{2,0,1:T(2,128)S(1)} %all_gather.24, f32[4,256,2048]{2,1,0:T(8,128)} %param.13, f32[2,4,256]{2,0,1:T(2,128)S(1)} %copy-done.49, f32[]{:T(128)} %bitcast, f32[4,256]{1,0:T(4,128)S(1)} %copy-done.53, ...), kind=kOutput, calls=%fused_computation.81 | convolution fusion | flops 50343936 | bytes 8511492 | tf_op jit(solution)/shard_map/lij,plj->pli/dot_general | solution.py:85
  161.4 12.6 %all-reduce.6 = (f32[2,160]{1,0:T(2,128)S(1)}, f32[2,4,40]{2,0,1:T(2,128)S(1)}) all-reduce(f32[2,160]{1,0:T(2,128)S(1)} %mul.639, f32[2,4,40]{2,0,1:T(2,128)S(1)} %copy.79), channel_id=1, replica_groups=mesh['inner'=4,'outer'=8] {'outer'}, use_global_device_ids=true, to_apply=%region_6.7 | all-reduce | flops 640 | bytes 5120 | tf_op jit(solution)/shard_map/psum | solution.py:42
  213.6 7.7 all_gather.25
  221.3 28.3 %reduce-scatter.27.cloned.1.call-done = f32[256,8]{1,0:T(8,128)} async-done(((f32[2048,8]{1,0:T(8,128)}), f32[256,8]{1,0:T(8,128)}) %reduce-scatter.27.cloned.1.call-update) | async-done | bytes 8208
  252.8 9.8 %fusion.50 = f32[2,4,256]{2,0,1:T(2,128)S(1)} fusion(f32[2,4,256]{2,0,1:T(2,128)S(1)} %fusion.62, f32[2,4,256]{2,0,1:T(2,128)S(1)} %copy.140, f32[2,5,2048]{2,0,1:T(2,128)S(1)} %all_gather.25, f32[4,256,2048]{2,1,0:T(8,128)} %param.13, f32[4,256]{1,0:T(4,128)S(1)} %get-tuple-element.129, f32[]{:T(128)} %bitcast, f32[4,256]{1,0:T(4,128)S(1)} %compare_convert_fusion, ...), kind=kOutput, calls=%fused_computation.75 | convolution fusion | flops 50345984 | bytes 8511492 | tf_op jit(solution)/shard_map/lij,plj->pli/dot_general | solution.py:85
  266.4 12.8 %all-reduce.5 = (f32[2,160]{1,0:T(2,128)}, f32[2,4,40]{2,0,1:T(2,128)S(1)}) all-reduce(f32[2,160]{1,0:T(2,128)S(1)} %mul.662, f32[2,4,40]{2,0,1:T(2,128)S(1)} %copy.83), channel_id=1, replica_groups=mesh['inner'=4,'outer'=8] {'outer'}, use_global_device_ids=true, to_apply=%region_9.10 | all-reduce | flops 640 | bytes 5120 | tf_op jit(solution)/shard_map/psum | solution.py:42
  296.6 8.4 %all_gather.26 = f32[2,5,2048]{2,0,1:T(2,128)S(1)} all-gather(f32[2,5,256]{2,0,1:T(2,128)S(1)} %pad_maximum_fusion.25), channel_id=1, replica_groups=mesh['inner'=4,'outer'=8] {'outer'}, dimensions={2}, use_global_device_ids=true | all-gather | bytes 92160 | tf_op jit(solution)/shard_map/all_gather | solution.py:83
  336.2 9.8 %fusion.45 = f32[2,4,256]{2,0,1:T(2,128)S(1)} fusion(f32[2,4,256]{2,0,1:T(2,128)S(1)} %fusion.61, f32[2,4,256]{2,0,1:T(2,128)S(1)} %copy.142, f32[2,5,2048]{2,0,1:T(2,128)S(1)} %all_gather.26, f32[4,256,2048]{2,1,0:T(8,128)} %param.13, f32[4,256]{1,0:T(4,128)S(1)} %get-tuple-element.130, f32[]{:T(128)} %bitcast, f32[4,256]{1,0:T(4,128)S(1)} %compare_convert_fusion, ...), kind=kOutput, calls=%fused_computation.69 | convolution fusion | flops 50345984 | bytes 8511492 | tf_op jit(solution)/shard_map/lij,plj->pli/dot_general | solution.py:85
  350.1 12.7 %all-reduce.4 = (f32[2,160]{1,0:T(2,128)}, f32[2,4,40]{2,0,1:T(2,128)S(1)}) all-reduce(f32[2,160]{1,0:T(2,128)S(1)} %mul.684, f32[2,4,40]{2,0,1:T(2,128)} %copy.87), channel_id=1, replica_groups=mesh['inner'=4,'outer'=8] {'outer'}, use_global_device_ids=true, to_apply=%region_12.13 | all-reduce | flops 640 | bytes 5120 | tf_op jit(solution)/shard_map/psum | solution.py:42
  380.6 8.0 all_gather.27
  388.6 28.1 %reduce-scatter.31.cloned.1.call-done = f32[256,8]{1,0:T(8,128)} async-done(((f32[2048,8]{1,0:T(8,128)}), f32[256,8]{1,0:T(8,128)}) %reduce-scatter.31.cloned.1.call-update) | async-done | bytes 8208
  419.8 9.8 %fusion.40 = f32[2,4,256]{2,0,1:T(2,128)S(1)} fusion(f32[2,4,256]{2,0,1:T(2,128)} %fusion.60, f32[2,4,256]{2,0,1:T(2,128)S(1)} %copy.144, f32[2,5,2048]{2,0,1:T(2,128)S(1)} %all_gather.27, f32[4,256,2048]{2,1,0:T(8,128)} %param.13, f32[4,256]{1,0:T(4,128)S(1)} %get-tuple-element.128, f32[]{:T(128)} %bitcast, f32[4,256]{1,0:T(4,128)S(1)} %compare_convert_fusion, ...), kind=kOutput, calls=%fused_computation.63 | convolution fusion | flops 50345984 | bytes 8511492 | tf_op jit(solution)/shard_map/lij,plj->pli/dot_general | solution.py:85
  453.2 8.3 all_gather.28
  472.7 14.2 %all-reduce.3 = (f32[2,160]{1,0:T(2,128)}, f32[2,4,40]{2,0,1:T(2,128)}) all-reduce(f32[2,160]{1,0:T(2,128)} %mul.704, f32[2,4,40]{2,0,1:T(2,128)S(1)} %copy.91), channel_id=1, replica_groups=mesh['inner'=4,'outer'=8] {'outer'}, use_global_device_ids=true, to_apply=%region_15.16 | all-reduce | flops 640 | bytes 5120 | tf_op jit(solution)/shard_map/psum | solution.py:42
  505.6 9.8 %fusion.35 = f32[2,4,256]{2,0,1:T(2,128)S(1)} fusion(f32[2,4,256]{2,0,1:T(2,128)} %fusion.59, f32[2,4,256]{2,0,1:T(2,128)} %copy.146, f32[2,5,2048]{2,0,1:T(2,128)S(1)} %all_gather.28, f32[4,256,2048]{2,1,0:T(8,128)} %param.13, f32[2,4,256]{2,0,1:T(2,128)S(1)} %fusion.196, f32[]{:T(128)} %bitcast.65, f32[4,256]{1,0:T(4,128)S(1)} %copy-done.53, ...), kind=kOutput, calls=%fused_computation.57 | convolution fusion | flops 50343936 | bytes 8511492 | tf_op jit(solution)/shard_map/lij,plj->pli/dot_general | solution.py:85
  523.5 6.8 convolution_bitcast_fusion.2
  538.8 7.5 all_gather.29
  557.7 14.5 %all-reduce.2 = (f32[2,160]{1,0:T(2,128)}, f32[2,4,40]{2,0,1:T(2,128)}) all-reduce(f32[2,160]{1,0:T(2,128)} %mul.721, f32[2,4,40]{2,0,1:T(2,128)S(1)} %copy.99), channel_id=1, replica_groups=mesh['inner'=4,'outer'=8] {'outer'}, use_global_device_ids=true, to_apply=%region_18.19 | all-reduce | flops 640 | bytes 5120 | tf_op jit(solution)/shard_map/psum | solution.py:42
  590.5 9.8 %fusion.30 = f32[2,4,256]{2,0,1:T(2,128)S(1)} fusion(f32[2,4,256]{2,0,1:T(2,128)} %fusion.58, f32[2,4,256]{2,0,1:T(2,128)} %copy.148, f32[2,5,2048]{2,0,1:T(2,128)S(1)} %all_gather.29, f32[4,256,2048]{2,1,0:T(8,128)} %param.13, f32[]{:T(128)} %bitcast.65, f32[4,256]{1,0:T(4,128)S(1)} %copy-done.55, f32[4,256]{1,0:T(4,128)S(1)} %compare_convert_fusion, ...), kind=kOutput, calls=%fused_computation.51 | convolution fusion | flops 50345984 | bytes 8511492 | tf_op jit(solution)/shard_map/lij,plj->pli/dot_general | solution.py:85
  623.7 7.7 all_gather.30
  631.3 28.7 %reduce-scatter.37.cloned.1.call-done = f32[256,8]{1,0:T(8,128)} async-done(((f32[2048,8]{1,0:T(8,128)}), f32[256,8]{1,0:T(8,128)}) %reduce-scatter.37.cloned.1.call-update) | async-done | bytes 8208
  677.2 13.2 %all-reduce.1 = (f32[2,160]{1,0:T(2,128)}, f32[2,4,40]{2,0,1:T(2,128)}) all-reduce(f32[2,160]{1,0:T(2,128)} %mul.738, f32[2,4,40]{2,0,1:T(2,128)} %copy.103), channel_id=1, replica_groups=mesh['inner'=4,'outer'=8] {'outer'}, use_global_device_ids=true, to_apply=%region_21.22 | all-reduce | flops 640 | bytes 5120 | tf_op jit(solution)/shard_map/psum | solution.py:42
  691.3 9.8 %fusion.25 = f32[2,4,256]{2,0,1:T(2,128)S(1)} fusion(f32[2,4,256]{2,0,1:T(2,128)S(1)} %fusion.57, f32[2,4,256]{2,0,1:T(2,128)} %copy.150, f32[2,5,2048]{2,0,1:T(2,128)S(1)} %all_gather.30, f32[4,256,2048]{2,1,0:T(8,128)} %param.13, f32[]{:T(128)} %bitcast.65, f32[4,256]{1,0:T(4,128)S(1)} %get-tuple-element.130, f32[4,256]{1,0:T(4,128)S(1)} %compare_convert_fusion, ...), kind=kOutput, calls=%fused_computation.45 | convolution fusion | flops 50345984 | bytes 8511492 | tf_op jit(solution)/shard_map/lij,plj->pli/dot_general | solution.py:85
  721.3 6.8 convolution_bitcast_fusion
  736.6 7.5 all_gather.31
  744.0 28.4 %reduce-scatter.39.cloned.1.call-done = f32[256,8]{1,0:T(8,128)} async-done(((f32[2048,8]{1,0:T(8,128)}), f32[256,8]{1,0:T(8,128)}) %reduce-scatter.39.cloned.1.call-update) | async-done | bytes 8208
  795.6 13.1 %all-reduce = (f32[2,4,40]{2,0,1:T(2,128)S(1)}, f32[2,160]{1,0:T(2,128)S(1)}) all-reduce(f32[2,4,40]{2,0,1:T(2,128)S(1)} %copy.107, f32[2,160]{1,0:T(2,128)S(1)} %mul.753), channel_id=1, replica_groups=mesh['inner'=4,'outer'=8] {'outer'}, use_global_device_ids=true, to_apply=%region_22.23 | all-reduce | flops 640 | bytes 5120 | tf_op jit(solution)/shard_map/psum | solution.py:20
  809.1 10.4 %fusion.20 = f32[2,4,256]{2,0,1:T(2,128)S(1)} fusion(f32[2,4,256]{2,0,1:T(2,128)S(1)} %fusion.56, f32[2,4,256]{2,0,1:T(2,128)S(1)} %copy.152, f32[2,5,2048]{2,0,1:T(2,128)S(1)} %all_gather.31, f32[4,256,2048]{2,1,0:T(8,128)} %param.13, f32[]{:T(128)} %bitcast.65, f32[4,256]{1,0:T(4,128)S(1)} %get-tuple-element.128, f32[4,256]{1,0:T(4,128)S(1)} %compare_convert_fusion, ...), kind=kOutput, calls=%fused_computation.39 | convolution fusion | flops 50345984 | bytes 8511492 | tf_op jit(solution)/shard_map/lij,plj->pli/dot_general | solution.py:85
  (484 shorter events, 404.5 us)
Async XLA Ops:
  7.2 140.7 %reduce-scatter.25.cloned.1.call-start = ((), (), s32[]{:S(2)}) async-start(), calls=%async_computation.8 | async-start | bytes 1179648
  8.7 88.7 %collective-permute-start.1 = (f32[2,256]{1,0:T(2,128)S(1)}, f32[2,256]{1,0:T(2,128)S(1)}, u32[]{:S(2)}, u32[]{:S(2)}) collective-permute-start(f32[2,256]{1,0:T(2,128)S(1)} %get-tuple-element.127), channel_id=1, source_target_pairs={{0,8},{8,16},{16,24},{1,9},{9,17},{17,25},{2,10},{10,18},{18,26},{... | collective-permute-start | bytes 6152 | tf_op jit(solution)/shard_map/ppermute | solution.py:15
  15.4 82.0 %collective-permute-start.2 = (f32[256,2048]{1,0:T(8,128)}, f32[256,2048]{1,0:T(8,128)S(1)}, u32[]{:S(2)}, u32[]{:S(2)}) collective-permute-start(f32[256,2048]{1,0:T(8,128)} %slice_bitcast_fusion), channel_id=1, source_target_pairs={{0,8},{8,16},{16,24},{1,9},{9,17},{17,25},{2,10},{10,18},{18,26},{... | collective-permute-start | bytes 6291464 | tf_op jit(solution)/shard_map/ppermute | solution.py:15
  88.5 85.4 %collective-permute-start.12 = (f32[2,160,1]{2,1,0:T(8,128)}, f32[2,160,1]{2,1,0:T(8,128)}, u32[]{:S(2)}, u32[]{:S(2)}) collective-permute-start(f32[2,160,1]{2,1,0:T(8,128)} %get-tuple-element.81), channel_id=1, source_target_pairs={{0,1},{1,2},{2,3},{3,4},{4,5},{5,6},{6,7},{8,9},{9,10},{10,11},{11... | collective-permute-start | bytes 3848 | tf_op jit(solution)/shard_map/ppermute | solution.py:31
  91.3 82.6 %collective-permute-start.13 = (f32[2,160,1]{2,1,0:T(8,128)}, f32[2,160,1]{2,1,0:T(8,128)}, u32[]{:S(2)}, u32[]{:S(2)}) collective-permute-start(f32[2,160,1]{2,1,0:T(8,128)} %get-tuple-element.82), channel_id=1, source_target_pairs={{1,0},{2,1},{3,2},{4,3},{5,4},{6,5},{7,6},{9,8},{10,9},{11,10},{12... | collective-permute-start | bytes 3848 | tf_op jit(solution)/shard_map/ppermute | solution.py:33
  113.7 135.9 %reduce-scatter.27.cloned.1.call-start = ((), (), s32[]{:S(2)}) async-start(), calls=%async_computation.9 | async-start | bytes 1179648
  186.0 119.1 %collective-permute-start.21 = (f32[2,40,512]{2,1,0:T(8,128)}, f32[2,40,512]{2,1,0:T(8,128)}, u32[]{:S(2)}, u32[]{:S(2)}) collective-permute-start(f32[2,40,512]{2,1,0:T(8,128)} %get-tuple-element.77), channel_id=1, source_target_pairs={{0,8},{8,16},{16,24},{1,9},{9,17},{17,25},{2,10},{10,18},{18,26},{... | collective-permute-start | bytes 491528 | tf_op jit(solution)/shard_map/ppermute | solution.py:15
  189.4 117.4 %collective-permute-start.20 = (f32[2,40,512]{2,1,0:T(8,128)}, f32[2,40,512]{2,1,0:T(8,128)}, u32[]{:S(2)}, u32[]{:S(2)}) collective-permute-start(f32[2,40,512]{2,1,0:T(8,128)} %get-tuple-element.76), channel_id=1, source_target_pairs={{8,0},{16,8},{24,16},{9,1},{17,9},{25,17},{10,2},{18,10},{26,18},{... | collective-permute-start | bytes 491528 | tf_op jit(solution)/shard_map/ppermute | solution.py:15
  192.5 116.8 %collective-permute-start.18 = (f32[2,160,1]{2,1,0:T(8,128)}, f32[2,160,1]{2,1,0:T(8,128)}, u32[]{:S(2)}, u32[]{:S(2)}) collective-permute-start(f32[2,160,1]{2,1,0:T(8,128)} %get-tuple-element.72), channel_id=1, source_target_pairs={{0,1},{1,2},{2,3},{3,4},{4,5},{5,6},{6,7},{8,9},{9,10},{10,11},{11... | collective-permute-start | bytes 3848 | tf_op jit(solution)/shard_map/ppermute | solution.py:31
  194.4 114.9 %collective-permute-start.19 = (f32[2,160,1]{2,1,0:T(8,128)}, f32[2,160,1]{2,1,0:T(8,128)}, u32[]{:S(2)}, u32[]{:S(2)}) collective-permute-start(f32[2,160,1]{2,1,0:T(8,128)} %get-tuple-element.73), channel_id=1, source_target_pairs={{1,0},{2,1},{3,2},{4,3},{5,4},{6,5},{7,6},{9,8},{10,9},{11,10},{12... | collective-permute-start | bytes 3848 | tf_op jit(solution)/shard_map/ppermute | solution.py:33
  213.5 119.4 %reduce-scatter.29.cloned.1.call-start = ((), (), s32[]{:S(2)}) async-start(), calls=%async_computation.10 | async-start | bytes 1179648
  296.6 120.0 %reduce-scatter.31.cloned.1.call-start = ((), (), s32[]{:S(2)}) async-start(), calls=%async_computation.11 | async-start | bytes 1179648
  315.8 145.7 %collective-permute-start.27 = (f32[2,40,512]{2,1,0:T(8,128)}, f32[2,40,512]{2,1,0:T(8,128)}, u32[]{:S(2)}, u32[]{:S(2)}) collective-permute-start(f32[2,40,512]{2,1,0:T(8,128)} %get-tuple-element.68), channel_id=1, source_target_pairs={{0,8},{8,16},{16,24},{1,9},{9,17},{17,25},{2,10},{10,18},{18,26},{... | collective-permute-start | bytes 491528 | tf_op jit(solution)/shard_map/ppermute | solution.py:15
  319.2 144.1 %collective-permute-start.26 = (f32[2,40,512]{2,1,0:T(8,128)}, f32[2,40,512]{2,1,0:T(8,128)}, u32[]{:S(2)}, u32[]{:S(2)}) collective-permute-start(f32[2,40,512]{2,1,0:T(8,128)} %get-tuple-element.67), channel_id=1, source_target_pairs={{8,0},{16,8},{24,16},{9,1},{17,9},{25,17},{10,2},{18,10},{26,18},{... | collective-permute-start | bytes 491528 | tf_op jit(solution)/shard_map/ppermute | solution.py:15
  322.3 143.5 %collective-permute-start.24 = (f32[2,160,1]{2,1,0:T(8,128)}, f32[2,160,1]{2,1,0:T(8,128)}, u32[]{:S(2)}, u32[]{:S(2)}) collective-permute-start(f32[2,160,1]{2,1,0:T(8,128)} %get-tuple-element.63), channel_id=1, source_target_pairs={{0,1},{1,2},{2,3},{3,4},{4,5},{5,6},{6,7},{8,9},{9,10},{10,11},{11... | collective-permute-start | bytes 3848 | tf_op jit(solution)/shard_map/ppermute | solution.py:31
  324.2 141.6 %collective-permute-start.25 = (f32[2,160,1]{2,1,0:T(8,128)}, f32[2,160,1]{2,1,0:T(8,128)}, u32[]{:S(2)}, u32[]{:S(2)}) collective-permute-start(f32[2,160,1]{2,1,0:T(8,128)} %get-tuple-element.64), channel_id=1, source_target_pairs={{1,0},{2,1},{3,2},{4,3},{5,4},{6,5},{7,6},{9,8},{10,9},{11,10},{12... | collective-permute-start | bytes 3848 | tf_op jit(solution)/shard_map/ppermute | solution.py:33
  380.5 121.3 %reduce-scatter.33.cloned.1.call-start = ((), (), s32[]{:S(2)}) async-start(), calls=%async_computation.12 | async-start | bytes 1179648
  453.1 133.5 %reduce-scatter.35.cloned.1.call-start = ((), (), s32[]{:S(2)}) async-start(), calls=%async_computation.13 | async-start | bytes 1179648
  488.4 57.9 %collective-permute-start.33 = (f32[2,40,512]{2,1,0:T(8,128)}, f32[2,40,512]{2,1,0:T(8,128)}, u32[]{:S(2)}, u32[]{:S(2)}) collective-permute-start(f32[2,40,512]{2,1,0:T(8,128)} %get-tuple-element.59), channel_id=1, source_target_pairs={{0,8},{8,16},{16,24},{1,9},{9,17},{17,25},{2,10},{10,18},{18,26},{... | collective-permute-start | bytes 491528 | tf_op jit(solution)/shard_map/ppermute | solution.py:15
  492.2 55.9 %collective-permute-start.32 = (f32[2,40,512]{2,1,0:T(8,128)}, f32[2,40,512]{2,1,0:T(8,128)}, u32[]{:S(2)}, u32[]{:S(2)}) collective-permute-start(f32[2,40,512]{2,1,0:T(8,128)} %get-tuple-element.58), channel_id=1, source_target_pairs={{8,0},{16,8},{24,16},{9,1},{17,9},{25,17},{10,2},{18,10},{26,18},{... | collective-permute-start | bytes 491528 | tf_op jit(solution)/shard_map/ppermute | solution.py:15
  494.9 55.7 %collective-permute-start.30 = (f32[2,160,1]{2,1,0:T(8,128)}, f32[2,160,1]{2,1,0:T(8,128)}, u32[]{:S(2)}, u32[]{:S(2)}) collective-permute-start(f32[2,160,1]{2,1,0:T(8,128)} %get-tuple-element.54), channel_id=1, source_target_pairs={{0,1},{1,2},{2,3},{3,4},{4,5},{5,6},{6,7},{8,9},{9,10},{10,11},{11... | collective-permute-start | bytes 3848 | tf_op jit(solution)/shard_map/ppermute | solution.py:31
  496.8 53.8 %collective-permute-start.31 = (f32[2,160,1]{2,1,0:T(8,128)}, f32[2,160,1]{2,1,0:T(8,128)}, u32[]{:S(2)}, u32[]{:S(2)}) collective-permute-start(f32[2,160,1]{2,1,0:T(8,128)} %get-tuple-element.55), channel_id=1, source_target_pairs={{1,0},{2,1},{3,2},{4,3},{5,4},{6,5},{7,6},{9,8},{10,9},{11,10},{12... | collective-permute-start | bytes 3848 | tf_op jit(solution)/shard_map/ppermute | solution.py:33
  538.1 122.0 %reduce-scatter.37.cloned.1.call-start = ((), (), s32[]{:S(2)}) async-start(), calls=%async_computation.14 | async-start | bytes 1179648
  573.7 90.2 %collective-permute-start.39 = (f32[2,40,512]{2,1,0:T(8,128)}, f32[2,40,512]{2,1,0:T(8,128)}, u32[]{:S(2)}, u32[]{:S(2)}) collective-permute-start(f32[2,40,512]{2,1,0:T(8,128)} %get-tuple-element.50), channel_id=1, source_target_pairs={{0,8},{8,16},{16,24},{1,9},{9,17},{17,25},{2,10},{10,18},{18,26},{... | collective-permute-start | bytes 491528 | tf_op jit(solution)/shard_map/ppermute | solution.py:15
  577.5 88.1 %collective-permute-start.38 = (f32[2,40,512]{2,1,0:T(8,128)}, f32[2,40,512]{2,1,0:T(8,128)}, u32[]{:S(2)}, u32[]{:S(2)}) collective-permute-start(f32[2,40,512]{2,1,0:T(8,128)} %get-tuple-element.49), channel_id=1, source_target_pairs={{8,0},{16,8},{24,16},{9,1},{17,9},{25,17},{10,2},{18,10},{26,18},{... | collective-permute-start | bytes 491528 | tf_op jit(solution)/shard_map/ppermute | solution.py:15
  580.2 88.0 %collective-permute-start.36 = (f32[2,160,1]{2,1,0:T(8,128)}, f32[2,160,1]{2,1,0:T(8,128)}, u32[]{:S(2)}, u32[]{:S(2)}) collective-permute-start(f32[2,160,1]{2,1,0:T(8,128)} %get-tuple-element.45), channel_id=1, source_target_pairs={{0,1},{1,2},{2,3},{3,4},{4,5},{5,6},{6,7},{8,9},{9,10},{10,11},{11... | collective-permute-start | bytes 3848 | tf_op jit(solution)/shard_map/ppermute | solution.py:31
  582.1 86.0 %collective-permute-start.37 = (f32[2,160,1]{2,1,0:T(8,128)}, f32[2,160,1]{2,1,0:T(8,128)}, u32[]{:S(2)}, u32[]{:S(2)}) collective-permute-start(f32[2,160,1]{2,1,0:T(8,128)} %get-tuple-element.46), channel_id=1, source_target_pairs={{1,0},{2,1},{3,2},{4,3},{5,4},{6,5},{7,6},{9,8},{10,9},{11,10},{12... | collective-permute-start | bytes 3848 | tf_op jit(solution)/shard_map/ppermute | solution.py:33
  622.9 149.5 %reduce-scatter.39.cloned.1.call-start = ((), (), s32[]{:S(2)}) async-start(), calls=%async_computation.15 | async-start | bytes 1179648
  706.0 67.8 %collective-permute-start.45 = (f32[2,40,512]{2,1,0:T(8,128)}, f32[2,40,512]{2,1,0:T(8,128)}, u32[]{:S(2)}, u32[]{:S(2)}) collective-permute-start(f32[2,40,512]{2,1,0:T(8,128)} %get-tuple-element.41), channel_id=1, source_target_pairs={{0,8},{8,16},{16,24},{1,9},{9,17},{17,25},{2,10},{10,18},{18,26},{... | collective-permute-start | bytes 491528 | tf_op jit(solution)/shard_map/ppermute | solution.py:15
  709.4 66.2 %collective-permute-start.44 = (f32[2,40,512]{2,1,0:T(8,128)}, f32[2,40,512]{2,1,0:T(8,128)}, u32[]{:S(2)}, u32[]{:S(2)}) collective-permute-start(f32[2,40,512]{2,1,0:T(8,128)} %get-tuple-element.40), channel_id=1, source_target_pairs={{8,0},{16,8},{24,16},{9,1},{17,9},{25,17},{10,2},{18,10},{26,18},{... | collective-permute-start | bytes 491528 | tf_op jit(solution)/shard_map/ppermute | solution.py:15
  712.5 65.6 %collective-permute-start.42 = (f32[2,160,1]{2,1,0:T(8,128)}, f32[2,160,1]{2,1,0:T(8,128)}, u32[]{:S(2)}, u32[]{:S(2)}) collective-permute-start(f32[2,160,1]{2,1,0:T(8,128)} %get-tuple-element.36), channel_id=1, source_target_pairs={{0,1},{1,2},{2,3},{3,4},{4,5},{5,6},{6,7},{8,9},{9,10},{10,11},{11... | collective-permute-start | bytes 3848 | tf_op jit(solution)/shard_map/ppermute | solution.py:31
  714.4 63.6 %collective-permute-start.43 = (f32[2,160,1]{2,1,0:T(8,128)}, f32[2,160,1]{2,1,0:T(8,128)}, u32[]{:S(2)}, u32[]{:S(2)}) collective-permute-start(f32[2,160,1]{2,1,0:T(8,128)} %get-tuple-element.37), channel_id=1, source_target_pairs={{1,0},{2,1},{3,2},{4,3},{5,4},{6,5},{7,6},{9,8},{10,9},{11,10},{12... | collective-permute-start | bytes 3848 | tf_op jit(solution)/shard_map/ppermute | solution.py:33
  (100 other events, 2209.3 us)
Sparse Core Ops, SparseCore 0:
  113.8 34.1 reduce-scatter.24
  213.6 35.9 reduce-scatter.26
  296.7 36.1 reduce-scatter.28
  380.6 35.9 reduce-scatter.30
  453.3 36.6 reduce-scatter.32
  538.2 36.7 reduce-scatter.34
  623.1 36.9 reduce-scatter.36
  736.0 36.3 reduce-scatter.38
where the time goes:
time: 847 us; the launch traced here: 835 us
  matrix products  174 us (21%)
  blocking collectives  169 us (20%)
  starting transfers between devices  156 us (18%)
  waiting for transfers between devices  152 us (18%)
  local copies, waits for them, and re-layouts  136 us (16%)
  other arithmetic  31.5 us (4%)
  between operations  17 us (2%)
    unnamed x16, waiting for transfers between devices  148 us
    ppermute x34, starting transfers between devices, from_behind(): return lax.ppermute(block, axis, route)  103 us
    unnamed x181, local copies, waits for them, and re-layouts  95.9 us
    psum x7, blocking collectives, reduce_partials(): boundary = lax.psum(partial_boundary, 'outer')  92.6 us
    dot_general x8, matrix products, local(): jnp.einsum('lij,plj->pli', dipole, gathered[:, 1:], precision=highest)  79.2 us
    all_gather x8, blocking collectives, local(): gathered = lax.all_gather(extended, 'outer', axis=2, tiled=True)  63.2 us
    dot_general x8, matrix products, local(): jnp.einsum('lji,plj->pli', source_blocks, source_rows, precision=highest)  55.2 us
    ppermute x8, starting transfers between devices, with_halo(): lax.ppermute(head, axis, [((i + 1) % count, i) for i in range(ends)])  36.4 us
  transfers between devices with their start and end apart: 58, of which 9 were waited for; matrix products, arithmetic and copies ran while one was open for 36% of the time, Pallas kernels for 0%

commit v1 on v0

--- a/solution.py
+++ b/solution.py
@@ -39,7 +39,7 @@
 
 def reduce_partials(partial_terms, partial_boundary):
     own_terms = lax.psum_scatter(partial_terms, "outer", scatter_dimension=2, tiled=True)
-    boundary = lax.psum(partial_boundary, "outer")
+    boundary = jnp.sum(lax.all_gather(partial_boundary, "outer"), axis=0)
     return (own_terms, boundary)
 
 

time: 847 us -> 892 us (1.053)
  blocking collectives: 169 us -> 189 us
  waiting for transfers between devices: 152 us -> 164 us
    psum x7 -> x0, blocking collectives: 92.6 us -> none  [reduce_partials(): boundary = lax.psum(partial_boundary, 'outer')]
    all_gather x0 -> x8, blocking collectives: none -> 65.1 us  [reduce_partials(): boundary = jnp.sum(lax.all_gather(partial_boundary, 'outer'), axis=0)]
    psum x1 -> x4, blocking collectives: 13.1 us -> 54.3 us  [spread(): return lax.psum(jnp.where(mine, shard, jnp.zeros_like(shard)), axis)]
    ppermute x34, waiting for transfers between devices: 3.96 us -> 14.9 us  [from_behind(): return lax.ppermute(block, axis, route)]
    unnamed x181 -> x161, local copies, waits for them, and re-layouts: 95.9 us -> 95.7 us
  transfers between devices with their start and end apart: 58 -> 58, of which waited for: 9 -> 9; matrix products, arithmetic and copies ran while one was open for 36% -> 34% of each run, Pallas kernels for 0% -> 0%
where the time goes in v1:
time: 892 us; the launch traced here: 881 us
  blocking collectives  189 us (21%)
  matrix products  177 us (20%)
  waiting for transfers between devices  164 us (18%)
  starting transfers between devices  154 us (17%)
  local copies, waits for them, and re-layouts  144 us (16%)
  other arithmetic  36 us (4%)
  between operations  16.5 us (2%)
    unnamed x16, waiting for transfers between devices  149 us
    ppermute x34, starting transfers between devices, from_behind(): return lax.ppermute(block, axis, route)  105 us
    unnamed x161, local copies, waits for them, and re-layouts  95.7 us
    dot_general x8, matrix products, local(): jnp.einsum('lij,plj->pli', dipole, gathered[:, 1:], precision=highest)  79.6 us
    all_gather x8, blocking collectives, local(): gathered = lax.all_gather(extended, 'outer', axis=2, tiled=True)  69.5 us
    all_gather x8, blocking collectives, reduce_partials(): boundary = jnp.sum(lax.all_gather(partial_boundary, 'outer'), axis=0)  65.1 us
    dot_general x8, matrix products, local(): jnp.einsum('lji,plj->pli', source_blocks, source_rows, precision=highest)  55.2 us
    psum x4, blocking collectives, spread(): return lax.psum(jnp.where(mine, shard, jnp.zeros_like(shard)), axis)  54.3 us
  transfers between devices with their start and end apart: 58, of which 9 were waited for; matrix products, arithmetic and copies ran while one was open for 34% of the time, Pallas kernels for 0%

profile of v1, /device:TPU:12, one launch (start us, length us, event | category | flops | bytes accessed | tf_op | source)
XLA Modules:
  0.0 881.0 jit_solution(4318822683819910728)
XLA Ops:
  44.0 9.1 %all-gather = f32[16,4,40]{2,1,0:T(4,128)S(1)} all-gather(f32[2,4,40]{2,1,0:T(4,128)S(1)} %copy.114), channel_id=2, replica_groups=mesh['inner'=4,'outer'=8] {'outer'}, dimensions={0}, use_global_device_ids=true | all-gather | bytes 11520 | tf_op jit(solution)/shard_map/all_gather | solution.py:42
  57.3 8.1 all_gather.72
  91.3 14.7 %all-reduce.3 = (f32[2,4,40]{2,0,1:T(2,128)S(1)}, f32[2,4,40]{2,0,1:T(2,128)S(1)}) all-reduce(f32[2,4,40]{2,0,1:T(2,128)S(1)} %copy.113, f32[2,4,40]{2,0,1:T(2,128)S(1)} %copy.125), channel_id=1, replica_groups=mesh['inner'=4,'outer'=8] {'outer'}, use_global_device_ids=true, to_apply=%region_1.2 | all-reduce | flops 640 | bytes 5120 | tf_op jit(solution)/shard_map/psum | solution.py:20
  108.4 14.2 %collective-permute-done.15 = f32[2,40,512]{2,1,0:T(8,128)} collective-permute-done((f32[2,40,512]{2,1,0:T(8,128)}, f32[2,40,512]{2,1,0:T(8,128)}, u32[]{:S(2)}, u32[]{:S(2)}) %collective-permute-start.15) | collective-permute-done | bytes 163872 | tf_op jit(solution)/shard_map/ppermute | solution.py:15
  147.7 32.4 %reduce-scatter.25.cloned.1.call-done = f32[256,8]{1,0:T(8,128)} async-done(((f32[2048,8]{1,0:T(8,128)}), f32[256,8]{1,0:T(8,128)}) %reduce-scatter.25.cloned.1.call-update) | async-done | bytes 8208
  183.3 9.9 %fusion.55 = f32[2,4,256]{2,0,1:T(2,128)S(1)} fusion(f32[2,4,256]{2,0,1:T(2,128)S(1)} %fusion.63, f32[2,4,256]{2,0,1:T(2,128)S(1)} %copy.198, f32[2,5,2048]{2,0,1:T(2,128)S(1)} %all_gather.72, f32[4,256,2048]{2,1,0:T(8,128)} %param.13, f32[2,4,256]{2,0,1:T(2,128)S(1)} %copy-done.44, f32[]{:T(128)} %bitcast, f32[4,256]{1,0:T(4,128)S(1)} %copy-done.46, ...), kind=kOutput, calls=%fused_computation.81 | convolution fusion | flops 50343936 | bytes 8511492 | tf_op jit(solution)/shard_map/lij,plj->pli/dot_general | solution.py:85
  193.5 8.2 all-gather.1
  241.2 8.0 all_gather.73
  249.2 26.6 %reduce-scatter.27.cloned.1.call-done = f32[256,8]{1,0:T(8,128)} async-done(((f32[2048,8]{1,0:T(8,128)}), f32[256,8]{1,0:T(8,128)}) %reduce-scatter.27.cloned.1.call-update) | async-done | bytes 8208
  279.0 9.9 %fusion.50 = f32[2,4,256]{2,0,1:T(2,128)S(1)} fusion(f32[2,4,256]{2,0,1:T(2,128)S(1)} %fusion.62, f32[2,4,256]{2,0,1:T(2,128)S(1)} %copy.200, f32[2,5,2048]{2,0,1:T(2,128)S(1)} %all_gather.73, f32[4,256,2048]{2,1,0:T(8,128)} %param.13, f32[4,256]{1,0:T(4,128)S(1)} %get-tuple-element.123, f32[]{:T(128)} %bitcast, f32[4,256]{1,0:T(4,128)S(1)} %compare_convert_fusion, ...), kind=kOutput, calls=%fused_computation.75 | convolution fusion | flops 50345984 | bytes 8511492 | tf_op jit(solution)/shard_map/lij,plj->pli/dot_general | solution.py:85
  292.6 8.2 all-gather.2
  318.8 8.9 %all_gather.76 = f32[2,5,2048]{2,0,1:T(2,128)S(1)} all-gather(f32[2,5,256]{2,0,1:T(2,128)S(1)} %pad_maximum_fusion.25), channel_id=1, replica_groups=mesh['inner'=4,'outer'=8] {'outer'}, dimensions={2}, use_global_device_ids=true | all-gather | bytes 92160 | tf_op jit(solution)/shard_map/all_gather | solution.py:83
  337.9 13.8 %all-reduce.2 = (f32[2,4,40]{2,0,1:T(2,128)S(1)}, f32[2,4,40]{2,0,1:T(2,128)S(1)}) all-reduce(f32[2,4,40]{2,0,1:T(2,128)S(1)} %copy-done.54, f32[2,4,40]{2,0,1:T(2,128)S(1)} %copy.137), channel_id=1, replica_groups=mesh['inner'=4,'outer'=8] {'outer'}, use_global_device_ids=true, to_apply=%region_7.8 | all-reduce | flops 640 | bytes 5120 | tf_op jit(solution)/shard_map/psum | solution.py:20
  369.3 9.9 %fusion.45 = f32[2,4,256]{2,0,1:T(2,128)S(1)} fusion(f32[2,4,256]{2,0,1:T(2,128)S(1)} %fusion.61, f32[2,4,256]{2,0,1:T(2,128)S(1)} %copy.202, f32[2,5,2048]{2,0,1:T(2,128)S(1)} %all_gather.76, f32[4,256,2048]{2,1,0:T(8,128)} %param.13, f32[4,256]{1,0:T(4,128)S(1)} %get-tuple-element.124, f32[]{:T(128)} %bitcast, f32[4,256]{1,0:T(4,128)S(1)} %compare_convert_fusion, ...), kind=kOutput, calls=%fused_computation.69 | convolution fusion | flops 50345984 | bytes 8511492 | tf_op jit(solution)/shard_map/lij,plj->pli/dot_general | solution.py:85
  407.7 10.2 %all_gather.79 = f32[2,5,2048]{2,0,1:T(2,128)S(1)} all-gather(f32[2,5,256]{2,0,1:T(2,128)S(1)} %pad_maximum_fusion.26), channel_id=1, replica_groups=mesh['inner'=4,'outer'=8] {'outer'}, dimensions={2}, use_global_device_ids=true | all-gather | bytes 92160 | tf_op jit(solution)/shard_map/all_gather | solution.py:83
  418.0 27.8 %reduce-scatter.31.cloned.1.call-done = f32[256,8]{1,0:T(8,128)} async-done(((f32[2048,8]{1,0:T(8,128)}), f32[256,8]{1,0:T(8,128)}) %reduce-scatter.31.cloned.1.call-update) | async-done | bytes 8208
  449.0 9.9 %fusion.40 = f32[2,4,256]{2,0,1:T(2,128)S(1)} fusion(f32[2,4,256]{2,0,1:T(2,128)} %fusion.60, f32[2,4,256]{2,0,1:T(2,128)S(1)} %copy.204, f32[2,5,2048]{2,0,1:T(2,128)S(1)} %all_gather.79, f32[4,256,2048]{2,1,0:T(8,128)} %param.13, f32[4,256]{1,0:T(4,128)S(1)} %get-tuple-element.122, f32[]{:T(128)} %bitcast, f32[4,256]{1,0:T(4,128)S(1)} %compare_convert_fusion, ...), kind=kOutput, calls=%fused_computation.63 | convolution fusion | flops 50345984 | bytes 8511492 | tf_op jit(solution)/shard_map/lij,plj->pli/dot_general | solution.py:85
  463.2 8.2 all-gather.4
  489.8 9.2 %all_gather.82 = f32[2,5,2048]{2,0,1:T(2,128)S(1)} all-gather(f32[2,5,256]{2,0,1:T(2,128)} %pad_maximum_fusion.27), channel_id=1, replica_groups=mesh['inner'=4,'outer'=8] {'outer'}, dimensions={2}, use_global_device_ids=true | all-gather | bytes 92160 | tf_op jit(solution)/shard_map/all_gather | solution.py:83
  542.7 12.7 %all-reduce.1 = (f32[2,4,40]{2,0,1:T(2,128)}, f32[2,4,40]{2,0,1:T(2,128)}) all-reduce(f32[2,4,40]{2,0,1:T(2,128)S(1)} %copy.143, f32[2,4,40]{2,0,1:T(2,128)} %copy.153), channel_id=1, replica_groups=mesh['inner'=4,'outer'=8] {'outer'}, use_global_device_ids=true, to_apply=%region_13.14 | all-reduce | flops 640 | bytes 5120 | tf_op jit(solution)/shard_map/psum | solution.py:20
  556.4 9.9 %fusion.35 = f32[2,4,256]{2,0,1:T(2,128)S(1)} fusion(f32[2,4,256]{2,0,1:T(2,128)S(1)} %fusion.59, f32[2,4,256]{2,0,1:T(2,128)} %copy.206, f32[2,5,2048]{2,0,1:T(2,128)S(1)} %all_gather.82, f32[4,256,2048]{2,1,0:T(8,128)} %param.13, f32[2,4,256]{2,0,1:T(2,128)S(1)} %fusion.196, f32[]{:T(128)} %bitcast.68, f32[4,256]{1,0:T(4,128)S(1)} %copy-done.46, ...), kind=kOutput, calls=%fused_computation.57 | convolution fusion | flops 50343936 | bytes 8511492 | tf_op jit(solution)/shard_map/lij,plj->pli/dot_general | solution.py:85
  575.7 8.2 all-gather.5
  621.2 26.9 %reduce-scatter.35.cloned.1.call-done = f32[256,8]{1,0:T(8,128)} async-done(((f32[2048,8]{1,0:T(8,128)}), f32[256,8]{1,0:T(8,128)}) %reduce-scatter.35.cloned.1.call-update) | async-done | bytes 8208
  651.9 9.9 %fusion.30 = f32[2,4,256]{2,0,1:T(2,128)S(1)} fusion(f32[2,4,256]{2,0,1:T(2,128)} %fusion.58, f32[2,4,256]{2,0,1:T(2,128)} %copy.208, f32[2,5,2048]{2,0,1:T(2,128)S(1)} %all_gather.85, f32[4,256,2048]{2,1,0:T(8,128)} %param.13, f32[]{:T(128)} %bitcast.68, f32[4,256]{1,0:T(4,128)S(1)} %copy-done.48, f32[4,256]{1,0:T(4,128)S(1)} %compare_convert_fusion, ...), kind=kOutput, calls=%fused_computation.51 | convolution fusion | flops 50345984 | bytes 8511492 | tf_op jit(solution)/shard_map/lij,plj->pli/dot_general | solution.py:85
  666.1 8.2 all-gather.6
  692.7 8.9 %all_gather.88 = f32[2,5,2048]{2,0,1:T(2,128)S(1)} all-gather(f32[2,5,256]{2,0,1:T(2,128)} %pad_maximum_fusion.29), channel_id=1, replica_groups=mesh['inner'=4,'outer'=8] {'outer'}, dimensions={2}, use_global_device_ids=true | all-gather | bytes 92160 | tf_op jit(solution)/shard_map/all_gather | solution.py:83
  747.5 13.0 %all-reduce = (f32[2,4,40]{2,0,1:T(2,128)}, f32[2,4,40]{2,0,1:T(2,128)}) all-reduce(f32[2,4,40]{2,0,1:T(2,128)} %copy.165, f32[2,4,40]{2,0,1:T(2,128)} %copy.159), channel_id=1, replica_groups=mesh['inner'=4,'outer'=8] {'outer'}, use_global_device_ids=true, to_apply=%region_22.23 | all-reduce | flops 640 | bytes 5120 | tf_op jit(solution)/shard_map/psum | solution.py:20
  761.4 9.9 %fusion.25 = f32[2,4,256]{2,0,1:T(2,128)S(1)} fusion(f32[2,4,256]{2,0,1:T(2,128)S(1)} %fusion.57, f32[2,4,256]{2,0,1:T(2,128)} %copy.210, f32[2,5,2048]{2,0,1:T(2,128)S(1)} %all_gather.88, f32[4,256,2048]{2,1,0:T(8,128)} %param.13, f32[]{:T(128)} %bitcast.68, f32[4,256]{1,0:T(4,128)S(1)} %get-tuple-element.124, f32[4,256]{1,0:T(4,128)S(1)} %compare_convert_fusion, ...), kind=kOutput, calls=%fused_computation.45 | convolution fusion | flops 50345984 | bytes 8511492 | tf_op jit(solution)/shard_map/lij,plj->pli/dot_general | solution.py:85
  772.7 8.1 all-gather.7
  816.6 8.3 all_gather.91
  824.8 28.2 %reduce-scatter.39.cloned.1.call-done = f32[256,8]{1,0:T(8,128)} async-done(((f32[2048,8]{1,0:T(8,128)}), f32[256,8]{1,0:T(8,128)}) %reduce-scatter.39.cloned.1.call-update) | async-done | bytes 8208
  854.6 10.4 %fusion.20 = f32[2,4,256]{2,0,1:T(2,128)S(1)} fusion(f32[2,4,256]{2,0,1:T(2,128)S(1)} %copy-done.53, f32[2,4,256]{2,0,1:T(2,128)S(1)} %copy.212, f32[2,5,2048]{2,0,1:T(2,128)S(1)} %all_gather.91, f32[4,256,2048]{2,1,0:T(8,128)} %param.13, f32[]{:T(128)} %bitcast.68, f32[4,256]{1,0:T(4,128)S(1)} %get-tuple-element.122, ...), kind=kOutput, calls=%fused_computation.39 | convolution fusion | flops 50345984 | bytes 8511492 | tf_op jit(solution)/shard_map/lij,plj->pli/dot_general | solution.py:85
  (476 shorter events, 454.8 us)
Async XLA Ops:
  7.2 172.9 %reduce-scatter.25.cloned.1.call-start = ((), (), s32[]{:S(2)}) async-start(), calls=%async_computation.8 | async-start | bytes 1179648
  9.2 56.2 %collective-permute-start.9 = (f32[40,40]{0,1:T(8,128)S(1)}, f32[40,40]{0,1:T(8,128)S(1)}, u32[]{:S(2)}, u32[]{:S(2)}) collective-permute-start(f32[40,40]{0,1:T(8,128)S(1)} %slice_bitcast_fusion.17), channel_id=1, source_target_pairs={{0,8},{8,16},{16,24},{1,9},{9,17},{17,25},{2,10},{10,18},{18,26},{... | collective-permute-start | bytes 19208 | tf_op jit(solution)/shard_map/ppermute | solution.py:15
  14.4 54.8 %collective-permute-start.8 = (f32[2,40,512]{2,1,0:T(8,128)S(1)}, f32[2,40,512]{2,1,0:T(8,128)}, u32[]{:S(2)}, u32[]{:S(2)}) collective-permute-start(f32[2,40,512]{2,1,0:T(8,128)S(1)} %get-tuple-element.89), channel_id=1, source_target_pairs={{0,8},{8,16},{16,24},{1,9},{9,17},{17,25},{2,10},{10,18},{18,26},{... | collective-permute-start | bytes 491528 | tf_op jit(solution)/shard_map/ppermute | solution.py:15
  17.9 56.0 %collective-permute-start.7 = (f32[2,40,512]{2,1,0:T(8,128)}, f32[2,40,512]{2,1,0:T(8,128)S(1)}, u32[]{:S(2)}, u32[]{:S(2)}) collective-permute-start(f32[2,40,512]{2,1,0:T(8,128)} %get-tuple-element.88), channel_id=1, source_target_pairs={{8,0},{16,8},{24,16},{9,1},{17,9},{25,17},{10,2},{18,10},{26,18},{... | collective-permute-start | bytes 491528 | tf_op jit(solution)/shard_map/ppermute | solution.py:15
  65.4 62.3 %collective-permute-start.1 = (f32[2,256]{1,0:T(2,128)}, f32[2,256]{1,0:T(2,128)S(1)}, u32[]{:S(2)}, u32[]{:S(2)}) collective-permute-start(f32[2,256]{1,0:T(2,128)} %get-tuple-element.121), channel_id=1, source_target_pairs={{0,8},{8,16},{16,24},{1,9},{9,17},{17,25},{2,10},{10,18},{18,26},{... | collective-permute-start | bytes 6152 | tf_op jit(solution)/shard_map/ppermute | solution.py:15
  69.2 58.5 %collective-permute-start.2 = (f32[256,2048]{1,0:T(8,128)}, f32[256,2048]{1,0:T(8,128)S(1)}, u32[]{:S(2)}, u32[]{:S(2)}) collective-permute-start(f32[256,2048]{1,0:T(8,128)} %slice_bitcast_fusion), channel_id=1, source_target_pairs={{0,8},{8,16},{16,24},{1,9},{9,17},{17,25},{2,10},{10,18},{18,26},{... | collective-permute-start | bytes 6291464 | tf_op jit(solution)/shard_map/ppermute | solution.py:15
  84.8 59.3 %collective-permute-start.14 = (f32[2,40,512]{2,1,0:T(8,128)}, f32[2,40,512]{2,1,0:T(8,128)}, u32[]{:S(2)}, u32[]{:S(2)}) collective-permute-start(f32[2,40,512]{2,1,0:T(8,128)} %get-tuple-element.82), channel_id=1, source_target_pairs={{8,0},{16,8},{24,16},{9,1},{17,9},{25,17},{10,2},{18,10},{26,18},{... | collective-permute-start | bytes 491528 | tf_op jit(solution)/shard_map/ppermute | solution.py:15
  89.4 112.4 %collective-permute-start.12 = (f32[2,160,1]{2,1,0:T(8,128)}, f32[2,160,1]{2,1,0:T(8,128)}, u32[]{:S(2)}, u32[]{:S(2)}) collective-permute-start(f32[2,160,1]{2,1,0:T(8,128)} %get-tuple-element.75), channel_id=1, source_target_pairs={{0,1},{1,2},{2,3},{3,4},{4,5},{5,6},{6,7},{8,9},{9,10},{10,11},{11... | collective-permute-start | bytes 3848 | tf_op jit(solution)/shard_map/ppermute | solution.py:31
  122.6 79.2 %collective-permute-start.13 = (f32[2,160,1]{2,1,0:T(8,128)}, f32[2,160,1]{2,1,0:T(8,128)}, u32[]{:S(2)}, u32[]{:S(2)}) collective-permute-start(f32[2,160,1]{2,1,0:T(8,128)} %get-tuple-element.76), channel_id=1, source_target_pairs={{1,0},{2,1},{3,2},{4,3},{5,4},{6,5},{7,6},{9,8},{10,9},{11,10},{12... | collective-permute-start | bytes 3848 | tf_op jit(solution)/shard_map/ppermute | solution.py:33
  144.0 131.8 %reduce-scatter.27.cloned.1.call-start = ((), (), s32[]{:S(2)}) async-start(), calls=%async_computation.9 | async-start | bytes 1179648
  212.0 115.7 %collective-permute-start.21 = (f32[2,40,512]{2,1,0:T(8,128)}, f32[2,40,512]{2,1,0:T(8,128)}, u32[]{:S(2)}, u32[]{:S(2)}) collective-permute-start(f32[2,40,512]{2,1,0:T(8,128)} %get-tuple-element.71), channel_id=1, source_target_pairs={{0,8},{8,16},{16,24},{1,9},{9,17},{17,25},{2,10},{10,18},{18,26},{... | collective-permute-start | bytes 491528 | tf_op jit(solution)/shard_map/ppermute | solution.py:15
  215.6 113.9 %collective-permute-start.20 = (f32[2,40,512]{2,1,0:T(8,128)}, f32[2,40,512]{2,1,0:T(8,128)}, u32[]{:S(2)}, u32[]{:S(2)}) collective-permute-start(f32[2,40,512]{2,1,0:T(8,128)} %get-tuple-element.70), channel_id=1, source_target_pairs={{8,0},{16,8},{24,16},{9,1},{17,9},{25,17},{10,2},{18,10},{26,18},{... | collective-permute-start | bytes 491528 | tf_op jit(solution)/shard_map/ppermute | solution.py:15
  219.5 112.6 %collective-permute-start.18 = (f32[2,160,1]{2,1,0:T(8,128)}, f32[2,160,1]{2,1,0:T(8,128)}, u32[]{:S(2)}, u32[]{:S(2)}) collective-permute-start(f32[2,160,1]{2,1,0:T(8,128)} %get-tuple-element.60), channel_id=1, source_target_pairs={{0,1},{1,2},{2,3},{3,4},{4,5},{5,6},{6,7},{8,9},{9,10},{10,11},{11... | collective-permute-start | bytes 3848 | tf_op jit(solution)/shard_map/ppermute | solution.py:31
  222.1 110.0 %collective-permute-start.19 = (f32[2,160,1]{2,1,0:T(8,128)}, f32[2,160,1]{2,1,0:T(8,128)}, u32[]{:S(2)}, u32[]{:S(2)}) collective-permute-start(f32[2,160,1]{2,1,0:T(8,128)} %get-tuple-element.61), channel_id=1, source_target_pairs={{1,0},{2,1},{3,2},{4,3},{5,4},{6,5},{7,6},{9,8},{10,9},{11,10},{12... | collective-permute-start | bytes 3848 | tf_op jit(solution)/shard_map/ppermute | solution.py:33
  241.1 125.0 %reduce-scatter.29.cloned.1.call-start = ((), (), s32[]{:S(2)}) async-start(), calls=%async_computation.10 | async-start | bytes 1179648
  318.7 127.1 %reduce-scatter.31.cloned.1.call-start = ((), (), s32[]{:S(2)}) async-start(), calls=%async_computation.11 | async-start | bytes 1179648
  352.7 146.3 %collective-permute-start.27 = (f32[2,40,512]{2,1,0:T(8,128)}, f32[2,40,512]{2,1,0:T(8,128)}, u32[]{:S(2)}, u32[]{:S(2)}) collective-permute-start(f32[2,40,512]{2,1,0:T(8,128)} %get-tuple-element.65), channel_id=1, source_target_pairs={{0,8},{8,16},{16,24},{1,9},{9,17},{17,25},{2,10},{10,18},{18,26},{... | collective-permute-start | bytes 491528 | tf_op jit(solution)/shard_map/ppermute | solution.py:15
  356.1 144.7 %collective-permute-start.26 = (f32[2,40,512]{2,1,0:T(8,128)}, f32[2,40,512]{2,1,0:T(8,128)}, u32[]{:S(2)}, u32[]{:S(2)}) collective-permute-start(f32[2,40,512]{2,1,0:T(8,128)} %get-tuple-element.64), channel_id=1, source_target_pairs={{8,0},{16,8},{24,16},{9,1},{17,9},{25,17},{10,2},{18,10},{26,18},{... | collective-permute-start | bytes 491528 | tf_op jit(solution)/shard_map/ppermute | solution.py:15
  359.2 144.2 %collective-permute-start.24 = (f32[2,160,1]{2,1,0:T(8,128)}, f32[2,160,1]{2,1,0:T(8,128)}, u32[]{:S(2)}, u32[]{:S(2)}) collective-permute-start(f32[2,160,1]{2,1,0:T(8,128)} %get-tuple-element.57), channel_id=1, source_target_pairs={{0,1},{1,2},{2,3},{3,4},{4,5},{5,6},{6,7},{8,9},{9,10},{10,11},{11... | collective-permute-start | bytes 3848 | tf_op jit(solution)/shard_map/ppermute | solution.py:31
  361.1 142.3 %collective-permute-start.25 = (f32[2,160,1]{2,1,0:T(8,128)}, f32[2,160,1]{2,1,0:T(8,128)}, u32[]{:S(2)}, u32[]{:S(2)}) collective-permute-start(f32[2,160,1]{2,1,0:T(8,128)} %get-tuple-element.58), channel_id=1, source_target_pairs={{1,0},{2,1},{3,2},{4,3},{5,4},{6,5},{7,6},{9,8},{10,9},{11,10},{12... | collective-permute-start | bytes 3848 | tf_op jit(solution)/shard_map/ppermute | solution.py:33
  407.7 119.6 %reduce-scatter.33.cloned.1.call-start = ((), (), s32[]{:S(2)}) async-start(), calls=%async_computation.12 | async-start | bytes 1179648
  489.7 158.4 %reduce-scatter.35.cloned.1.call-start = ((), (), s32[]{:S(2)}) async-start(), calls=%async_computation.13 | async-start | bytes 1179648
  584.5 117.1 %collective-permute-start.39 = (f32[2,40,512]{2,1,0:T(8,128)}, f32[2,40,512]{2,1,0:T(8,128)}, u32[]{:S(2)}, u32[]{:S(2)}) collective-permute-start(f32[2,40,512]{2,1,0:T(8,128)} %get-tuple-element.47), channel_id=1, source_target_pairs={{0,8},{8,16},{16,24},{1,9},{9,17},{17,25},{2,10},{10,18},{18,26},{... | collective-permute-start | bytes 491528 | tf_op jit(solution)/shard_map/ppermute | solution.py:15
  588.9 114.5 %collective-permute-start.38 = (f32[2,40,512]{2,1,0:T(8,128)}, f32[2,40,512]{2,1,0:T(8,128)}, u32[]{:S(2)}, u32[]{:S(2)}) collective-permute-start(f32[2,40,512]{2,1,0:T(8,128)} %get-tuple-element.46), channel_id=1, source_target_pairs={{8,0},{16,8},{24,16},{9,1},{17,9},{25,17},{10,2},{18,10},{26,18},{... | collective-permute-start | bytes 491528 | tf_op jit(solution)/shard_map/ppermute | solution.py:15
  591.0 115.0 %collective-permute-start.36 = (f32[2,160,1]{2,1,0:T(8,128)}, f32[2,160,1]{2,1,0:T(8,128)}, u32[]{:S(2)}, u32[]{:S(2)}) collective-permute-start(f32[2,160,1]{2,1,0:T(8,128)} %get-tuple-element.39), channel_id=1, source_target_pairs={{0,1},{1,2},{2,3},{3,4},{4,5},{5,6},{6,7},{8,9},{9,10},{10,11},{11... | collective-permute-start | bytes 3848 | tf_op jit(solution)/shard_map/ppermute | solution.py:31
  593.0 113.0 %collective-permute-start.37 = (f32[2,160,1]{2,1,0:T(8,128)}, f32[2,160,1]{2,1,0:T(8,128)}, u32[]{:S(2)}, u32[]{:S(2)}) collective-permute-start(f32[2,160,1]{2,1,0:T(8,128)} %get-tuple-element.40), channel_id=1, source_target_pairs={{1,0},{2,1},{3,2},{4,3},{5,4},{6,5},{7,6},{9,8},{10,9},{11,10},{12... | collective-permute-start | bytes 3848 | tf_op jit(solution)/shard_map/ppermute | solution.py:33
  612.5 117.8 %reduce-scatter.37.cloned.1.call-start = ((), (), s32[]{:S(2)}) async-start(), calls=%async_computation.14 | async-start | bytes 1179648
  692.7 160.4 %reduce-scatter.39.cloned.1.call-start = ((), (), s32[]{:S(2)}) async-start(), calls=%async_computation.15 | async-start | bytes 1179648
  781.0 84.7 %collective-permute-start.49 = (f32[2,40,512]{2,1,0:T(8,128)}, f32[2,40,512]{2,1,0:T(8,128)}, u32[]{:S(2)}, u32[]{:S(2)}) collective-permute-start(f32[2,40,512]{2,1,0:T(8,128)} %get-tuple-element.23), channel_id=1, source_target_pairs={{0,8},{8,16},{16,24},{1,9},{9,17},{17,25},{2,10},{10,18},{18,26},{... | collective-permute-start | bytes 491528 | tf_op jit(solution)/shard_map/ppermute | solution.py:15
  785.0 82.5 %collective-permute-start.48 = (f32[2,40,512]{2,1,0:T(8,128)}, f32[2,40,512]{2,1,0:T(8,128)}, u32[]{:S(2)}, u32[]{:S(2)}) collective-permute-start(f32[2,40,512]{2,1,0:T(8,128)} %get-tuple-element.22), channel_id=1, source_target_pairs={{8,0},{16,8},{24,16},{9,1},{17,9},{25,17},{10,2},{18,10},{26,18},{... | collective-permute-start | bytes 491528 | tf_op jit(solution)/shard_map/ppermute | solution.py:15
  787.5 82.5 %collective-permute-start.46 = (f32[2,160,1]{2,1,0:T(8,128)}, f32[2,160,1]{2,1,0:T(8,128)}, u32[]{:S(2)}, u32[]{:S(2)}) collective-permute-start(f32[2,160,1]{2,1,0:T(8,128)} %get-tuple-element.24), channel_id=1, source_target_pairs={{0,1},{1,2},{2,3},{3,4},{4,5},{5,6},{6,7},{8,9},{9,10},{10,11},{11... | collective-permute-start | bytes 3848 | tf_op jit(solution)/shard_map/ppermute | solution.py:31
  789.4 80.6 %collective-permute-start.47 = (f32[2,160,1]{2,1,0:T(8,128)}, f32[2,160,1]{2,1,0:T(8,128)}, u32[]{:S(2)}, u32[]{:S(2)}) collective-permute-start(f32[2,160,1]{2,1,0:T(8,128)} %get-tuple-element.26), channel_id=1, source_target_pairs={{1,0},{2,1},{3,2},{4,3},{5,4},{6,5},{7,6},{9,8},{10,9},{11,10},{12... | collective-permute-start | bytes 3848 | tf_op jit(solution)/shard_map/ppermute | solution.py:33
  (90 other events, 1917.9 us)
Sparse Core Ops, SparseCore 0:
  144.1 35.8 reduce-scatter.24
  241.3 34.4 reduce-scatter.26
  318.9 37.0 reduce-scatter.28
  407.8 37.9 reduce-scatter.30
  489.8 37.4 reduce-scatter.32
  612.6 35.4 reduce-scatter.34
  692.8 37.4 reduce-scatter.36
  816.0 37.0 reduce-scatter.38
